TPU v7x, 32 devices: a whole 2x2x4 slice. The times are simulated.
32 devices in a mesh: dp: 8 (over z, x), tensor: 4 (over y, core).
Axes of the slice: x: 2, y: 2, z: 4, core: 2. Of those that a mesh axis runs over, the one named last changes fastest.
Arguments:
- residual_in: float32 [16384, 768], P(('dp', 'tensor')), may hold values from -6 to 6
- out_grad: float32 [16384, 768], P(('dp', 'tensor')), may hold values from -6 to 6
- seq_lengths: int32 [8, 16], P('dp'), may hold values from 0 to 1024, as said below
- timesteps: int32 [8, 16], P('dp'), may hold values from 0 to 1023
- norm_gain: float32 [768], replicated, may hold values from 0.5 to 1.5
- norm_bias: float32 [768], replicated, may hold values from -3 to 3
- qkv_weight: float32 [3, 768, 768], P(None, 'dp', 'tensor'), may hold values from -0.21875 to 0.21875
- proj_weight: float32 [768, 768], P('tensor', 'dp'), may hold values from -0.875 to 0.875
- proj_bias: float32 [768], replicated, may hold values from -2 to 2
- up_weight: float32 [768, 3072], P('dp', 'tensor'), may hold values from -0.21875 to 0.21875
- up_bias: float32 [3072], replicated, may hold values from -3 to 3
- down_weight: float32 [3072, 768], P('tensor', 'dp'), may hold values from -0.109375 to 0.109375
- down_bias: float32 [768], replicated, may hold values from -2 to 2
- time_weight: float32 [128, 2304], replicated, may hold values from -0.5 to 0.5
- time_bias: float32 [2304], replicated, may hold values from -3 to 3
Outputs:
- residual_out: float32 [16384, 768], P(('dp', 'tensor'))
- input_grad: float32 [16384, 768], P(('dp', 'tensor'))
- norm_gain_grad: float32 [768], replicated
- norm_bias_grad: float32 [768], replicated
- qkv_weight_grad: float32 [3, 768, 768], P(None, 'dp', 'tensor')
- proj_weight_grad: float32 [768, 768], P('tensor', 'dp')
- proj_bias_grad: float32 [768], replicated
- up_weight_grad: float32 [768, 3072], P('dp', 'tensor')
- up_bias_grad: float32 [3072], replicated
- down_weight_grad: float32 [3072, 768], P('tensor', 'dp')
- down_bias_grad: float32 [768], replicated
- time_weight_grad: float32 [128, 2304], replicated
- time_bias_grad: float32 [2304], replicated
Inputs may be any that keep to these rules, and one draw needn't show every extreme that they name: `seq_lengths`: row g lists the lengths of the sequences packed in order into the 2048 rows of pack g: the nonzero lengths come first and lie between 128 and 1024, their sum is at most 2048, the rows after it are padding, and every row holds a length of exactly 1024.
All inputs are finite; a program needn't handle non-finite values.
Results may differ from a plain program's by a relative error of at most 0.015.
Values may be sent and summed in bfloat16 or wider, within the bound.
A program may use at most 128 MiB of HBM per device.

v0:
```python
import math
import jax
import jax.numpy as jnp
from jax import lax
from jax.sharding import PartitionSpec as P

HDIM = 64
QBLK = 512
highest = lax.Precision.HIGHEST


def normalize(values):
    center = values - jnp.mean(values, axis=-1, keepdims=True)
    inverse = lax.rsqrt(jnp.mean(center * center, axis=-1, keepdims=True) + 1e-05)
    return (center * inverse, inverse)


def norm_back(grad_in, normed, inverse):
    return inverse * (
        grad_in
        - jnp.mean(grad_in, axis=-1, keepdims=True)
        - normed * jnp.mean(grad_in * normed, axis=-1, keepdims=True)
    )


def pack_info(lengths, row_total):
    row_index = jnp.arange(row_total, dtype=jnp.int32)
    seq_ends = jnp.cumsum(lengths)
    passed = row_index[:, None] >= seq_ends[None, :]
    segment = jnp.sum(passed.astype(jnp.int32), axis=1)
    starts = jnp.sum(jnp.where(passed, lengths[None, :], 0), axis=1)
    return (segment, row_index - starts)


def time_embed(time_index, embed_width):
    half_width = embed_width // 2
    freqs = jnp.exp(-math.log(10000.0) * jnp.arange(half_width, dtype=jnp.float32) / half_width)
    angles = time_index.astype(jnp.float32)[:, None] * freqs[None, :]
    return jnp.concatenate([jnp.cos(angles), jnp.sin(angles)], axis=1)


def rope_tables(positions, head_width):
    half_width = head_width // 2
    inverse = jnp.exp(
        -math.log(10000.0) * jnp.arange(half_width, dtype=jnp.float32) * (2.0 / head_width)
    )
    angles = positions.astype(jnp.float32)[:, None] * inverse[None, :]
    return (jnp.cos(angles)[:, None, :], jnp.sin(angles)[:, None, :])


def rotate(values, cosine, sine_table):
    half_width = values.shape[-1] // 2
    lead_half = values[..., :half_width]
    tail_half = values[..., half_width:]
    return jnp.concatenate(
        [lead_half * cosine - tail_half * sine_table, tail_half * cosine + lead_half * sine_table],
        axis=-1,
    )


def masked_scores(query_block, segment_block, keys_low, segment):
    scores = jnp.einsum("qhd,khd->hqk", query_block, keys_low, preferred_element_type=jnp.float32)
    allowed = segment_block[:, None] == segment[None, :]
    return jnp.where(allowed[None], scores, -1000000000.0)


def gelu_tanh(values):
    return jax.nn.gelu(values, approximate=True)


def shards(
    residual_in,
    out_grad,
    seq_lengths,
    timesteps,
    norm_gain,
    norm_bias,
    qkv_weight,
    proj_weight,
    proj_bias,
    up_weight,
    up_bias,
    down_weight,
    down_bias,
    time_weight,
    time_bias,
):
    row_count = residual_in.shape[0]
    width_model = residual_in.shape[1]
    tensor_size = lax.axis_size("tensor")
    tensor_rank = lax.axis_index("tensor")
    total_rows = row_count * tensor_size
    own_offset = tensor_rank * row_count
    segment, positions = pack_info(seq_lengths[0], total_rows)
    slot_count = seq_lengths.shape[1]
    own_segment = lax.dynamic_slice_in_dim(segment, own_offset, row_count)
    onehot = (own_segment[:, None] == jnp.arange(slot_count, dtype=jnp.int32)[None, :]).astype(
        jnp.float32
    )
    embedded = time_embed(timesteps[0], time_weight.shape[0])
    mod_table = jnp.dot(embedded, time_weight, precision=highest) + time_bias
    modulation = jnp.dot(onehot, mod_table, precision=highest)
    mod_scale = modulation[:, :width_model]
    mod_shift = modulation[:, width_model : 2 * width_model]
    mod_gate = modulation[:, 2 * width_model :]
    gathered_qkv, gathered_proj, gathered_up, gathered_down = (
        lax.all_gather(qkv_weight.astype(jnp.bfloat16), "dp", axis=1, tiled=True),
        lax.all_gather(proj_weight.astype(jnp.bfloat16), "dp", axis=1, tiled=True),
        lax.all_gather(up_weight.astype(jnp.bfloat16), "dp", axis=0, tiled=True),
        lax.all_gather(down_weight.astype(jnp.bfloat16), "dp", axis=1, tiled=True),
    )
    local_heads = gathered_qkv.shape[2] // HDIM
    local_units = gathered_up.shape[1]
    normed_in, inverse_in = normalize(residual_in)
    normed_low = (normed_in * norm_gain + norm_bias).astype(jnp.bfloat16)
    normed_full = lax.all_gather(normed_low, "tensor", axis=0, tiled=True)
    projected = jnp.einsum(
        "td,cde->cte", normed_full, gathered_qkv, preferred_element_type=jnp.float32
    )
    cosine, sine_table = rope_tables(positions, HDIM)
    head_scale = 1.0 / math.sqrt(HDIM)
    queries_low = (
        rotate(projected[0].reshape(total_rows, local_heads, HDIM), cosine, sine_table) * head_scale
    ).astype(jnp.bfloat16)
    keys_low = rotate(
        projected[1].reshape(total_rows, local_heads, HDIM), cosine, sine_table
    ).astype(jnp.bfloat16)
    values_low = projected[2].reshape(total_rows, local_heads, HDIM).astype(jnp.bfloat16)
    block_count = total_rows // QBLK
    query_blocks = queries_low.reshape(block_count, QBLK, local_heads, HDIM)
    segment_blocks = segment.reshape(block_count, QBLK)

    def forward_block(block_item):
        query_block, segment_block = block_item
        scores = masked_scores(query_block, segment_block, keys_low, segment)
        row_max = jnp.max(scores, axis=-1, keepdims=True)
        exponent = jnp.exp(scores - row_max)
        row_total = jnp.sum(exponent, axis=-1, keepdims=True)
        soft_weights = exponent / row_total
        mixed = jnp.einsum(
            "hqk,khd->qhd",
            soft_weights.astype(jnp.bfloat16),
            values_low,
            preferred_element_type=jnp.float32,
        )
        return (mixed.astype(jnp.bfloat16), (row_max + jnp.log(row_total))[..., 0])

    mixed_blocks, log_totals = lax.map(forward_block, (query_blocks, segment_blocks))
    mixed_flat = mixed_blocks.reshape(total_rows, local_heads * HDIM)
    attention = lax.psum_scatter(
        jnp.dot(mixed_flat, gathered_proj, preferred_element_type=jnp.float32).astype(jnp.bfloat16),
        "tensor",
        scatter_dimension=0,
        tiled=True,
    ).astype(jnp.float32)
    hidden = residual_in + attention + proj_bias
    hidden_normed, inverse_hidden = normalize(hidden)
    modulated_low = (hidden_normed * (1.0 + mod_scale) + mod_shift).astype(jnp.bfloat16)
    branch_grad = out_grad * mod_gate
    modulated_full = lax.all_gather(modulated_low, "tensor", axis=0, tiled=True)
    up_bias_own = lax.dynamic_slice_in_dim(up_bias, tensor_rank * local_units, local_units)
    pre_act = jnp.dot(modulated_full, gathered_up, preferred_element_type=jnp.float32) + up_bias_own
    active, gelu_pullback = jax.vjp(gelu_tanh, pre_act)
    active_low = active.astype(jnp.bfloat16)
    down_sum = lax.psum_scatter(
        jnp.dot(active_low, gathered_down, preferred_element_type=jnp.float32).astype(jnp.bfloat16),
        "tensor",
        scatter_dimension=0,
        tiled=True,
    ).astype(jnp.float32)
    branch = down_sum + down_bias
    residual_out = hidden + mod_gate * branch
    gate_grad = out_grad * branch
    branch_full = lax.all_gather(branch_grad.astype(jnp.bfloat16), "tensor", axis=0, tiled=True)
    down_part = lax.dot_general(
        active_low, branch_full, (((0,), (0,)), ((), ())), preferred_element_type=jnp.float32
    )
    active_grad = lax.dot_general(
        branch_full, gathered_down, (((1,), (1,)), ((), ())), preferred_element_type=jnp.float32
    )
    pre_grad = gelu_pullback(active_grad)[0].astype(jnp.bfloat16)
    up_bias_own_part = jnp.sum(pre_grad, axis=0, dtype=jnp.float32)
    up_bias_part = lax.dynamic_update_slice_in_dim(
        jnp.zeros(up_bias.shape, jnp.float32), up_bias_own_part, tensor_rank * local_units, 0
    )
    up_part = lax.dot_general(
        modulated_full, pre_grad, (((0,), (0,)), ((), ())), preferred_element_type=jnp.float32
    )
    modulated_grad = lax.psum_scatter(
        lax.dot_general(
            pre_grad, gathered_up, (((1,), (1,)), ((), ())), preferred_element_type=jnp.float32
        ).astype(jnp.bfloat16),
        "tensor",
        scatter_dimension=0,
        tiled=True,
    ).astype(jnp.float32)
    down_bias_part = jnp.sum(branch_grad, axis=0)
    scale_grad = modulated_grad * hidden_normed
    hidden_norm_grad = modulated_grad * (1.0 + mod_scale)
    hidden_grad = out_grad + norm_back(hidden_norm_grad, hidden_normed, inverse_hidden)
    mod_grad = jnp.concatenate([scale_grad, modulated_grad, gate_grad], axis=1)
    mod_seq_grad = lax.dot_general(onehot, mod_grad, (((0,), (0,)), ((), ())), precision=highest)
    time_weight_part = lax.dot_general(
        embedded, mod_seq_grad, (((0,), (0,)), ((), ())), precision=highest
    )
    time_bias_part = jnp.sum(mod_seq_grad, axis=0)
    proj_bias_part = jnp.sum(hidden_grad, axis=0)
    hidden_full = lax.all_gather(hidden_grad.astype(jnp.bfloat16), "tensor", axis=0, tiled=True)
    proj_part = lax.dot_general(
        mixed_flat, hidden_full, (((0,), (0,)), ((), ())), preferred_element_type=jnp.float32
    )
    mixed_grad = lax.dot_general(
        hidden_full, gathered_proj, (((1,), (1,)), ((), ())), preferred_element_type=jnp.float32
    )
    grad_blocks = mixed_grad.astype(jnp.bfloat16).reshape(block_count, QBLK, local_heads, HDIM)

    def backward_block(carried, block_item):
        key_sum, value_sum = carried
        query_block, segment_block, log_block, grad_block = block_item
        scores = masked_scores(query_block, segment_block, keys_low, segment)
        soft_weights = jnp.exp(scores - log_block[:, :, None])
        prob_grad = jnp.einsum(
            "qhd,khd->hqk", grad_block, values_low, preferred_element_type=jnp.float32
        )
        row_inner = jnp.sum(soft_weights * prob_grad, axis=-1, keepdims=True)
        score_grad = (soft_weights * (prob_grad - row_inner)).astype(jnp.bfloat16)
        query_grad = jnp.einsum(
            "hqk,khd->qhd", score_grad, keys_low, preferred_element_type=jnp.float32
        )
        key_sum = key_sum + jnp.einsum(
            "hqk,qhd->khd", score_grad, query_block, preferred_element_type=jnp.float32
        )
        value_sum = value_sum + jnp.einsum(
            "hqk,qhd->khd",
            soft_weights.astype(jnp.bfloat16),
            grad_block,
            preferred_element_type=jnp.float32,
        )
        return ((key_sum, value_sum), query_grad)

    empty_grad = jnp.zeros((total_rows, local_heads, HDIM), jnp.float32)
    (key_grad, value_grad), query_grads = lax.scan(
        backward_block,
        (empty_grad, empty_grad),
        (query_blocks, segment_blocks, log_totals, grad_blocks),
    )
    query_grad_all = query_grads.reshape(total_rows, local_heads, HDIM)
    query_raw_grad = rotate(query_grad_all * head_scale, cosine, -sine_table)
    key_raw_grad = rotate(key_grad, cosine, -sine_table)
    qkv_grad = (
        jnp.stack([query_raw_grad, key_raw_grad, value_grad])
        .reshape(3, total_rows, local_heads * HDIM)
        .astype(jnp.bfloat16)
    )
    qkv_part = jnp.einsum("td,cte->cde", normed_full, qkv_grad, preferred_element_type=jnp.float32)
    normed_grad = lax.psum_scatter(
        jnp.einsum(
            "cte,cde->td", qkv_grad, gathered_qkv, preferred_element_type=jnp.float32
        ).astype(jnp.bfloat16),
        "tensor",
        scatter_dimension=0,
        tiled=True,
    ).astype(jnp.float32)
    gain_part = jnp.sum(normed_grad * normed_in, axis=0)
    bias_part = jnp.sum(normed_grad, axis=0)
    input_grad = hidden_grad + norm_back(normed_grad * norm_gain, normed_in, inverse_in)
    grad_qkv, grad_proj, grad_up, grad_down = (
        lax.psum_scatter(qkv_part, "dp", scatter_dimension=1, tiled=True),
        lax.psum_scatter(proj_part, "dp", scatter_dimension=1, tiled=True),
        lax.psum_scatter(up_part, "dp", scatter_dimension=0, tiled=True),
        lax.psum_scatter(down_part, "dp", scatter_dimension=1, tiled=True),
    )
    small_sums = lax.psum(
        (
            gain_part,
            bias_part,
            proj_bias_part,
            up_bias_part,
            down_bias_part,
            time_weight_part,
            time_bias_part,
        ),
        ("dp", "tensor"),
    )
    return (
        residual_out,
        input_grad,
        small_sums[0],
        small_sums[1],
        grad_qkv,
        grad_proj,
        small_sums[2],
        grad_up,
        small_sums[3],
        grad_down,
        small_sums[4],
        small_sums[5],
        small_sums[6],
    )


def solution(mesh):
    in_specs = (
        P(("dp", "tensor"), None),
        P(("dp", "tensor"), None),
        P("dp", None),
        P("dp", None),
        P(),
        P(),
        P(None, "dp", "tensor"),
        P("tensor", "dp"),
        P(),
        P("dp", "tensor"),
        P(),
        P("tensor", "dp"),
        P(),
        P(),
        P(),
    )
    out_specs = (
        P(("dp", "tensor"), None),
        P(("dp", "tensor"), None),
        P(),
        P(),
        P(None, "dp", "tensor"),
        P("tensor", "dp"),
        P(),
        P("dp", "tensor"),
        P(),
        P("tensor", "dp"),
        P(),
        P(),
        P(),
    )
    return jax.shard_map(shards, mesh=mesh, in_specs=in_specs, out_specs=out_specs, check_vma=False)
```

profile of v0, /device:TPU:0, one launch (start us, length us, event | category | flops | bytes accessed | tf_op | source)
XLA Modules:
  0.0 983.2 jit_solution(7752783415744753247)
XLA Ops:
  12.9 40.6 %all_gather.25 = bf16[3,768,192]{2,0,1:T(4,128)(2,1)} all-gather(bf16[3,96,192]{2,0,1:T(4,128)(2,1)S(1)} %copy.65), channel_id=1, replica_groups=mesh['dp'=8,'tensor'=4] {'dp'}, dimensions={1}, use_global_device_ids=true | all-gather | bytes 995328 | tf_op jit(solution)/shard_map/all_gather | solution.py:107
  57.0 33.0 %all_gather.26 = bf16[192,768]{0,1:T(8,128)(2,1)} all-gather(bf16[192,96]{0,1:T(8,128)(2,1)S(1)} %copy.69), channel_id=1, replica_groups=mesh['dp'=8,'tensor'=4] {'dp'}, dimensions={1}, use_global_device_ids=true | all-gather | bytes 331776 | tf_op jit(solution)/shard_map/all_gather | solution.py:108
  106.1 95.3 %while.27 = (s32[]{:T(128)}, bf16[4,512,3,64]{1,3,2,0:T(8,128)(2,1)}, f32[4,3,512]{2,1,0:T(4,128)}, s32[4,512]{1,0:T(4,128)S(1)}, s32[2048]{0:T(1024)S(1)}, /*in...) while((s32[]{:T(128)}, ...), condition=%wide.region_8.9_spmd, body=%wide.region_5.8_spmd.sunk | while | flops 834763264 | bytes 47120528 | solution.py:148
  114.6 7.8 fusion.140
  185.8 7.8 fusion.140
  218.0 26.7 %reduce-scatter.13.cloned.1.call-done = bf16[512,768]{1,0:T(8,128)(2,1)} async-done(((bf16[2048,768]{1,0:T(8,128)(2,1)}), bf16[512,768]{1,0:T(8,128)(2,1)}) %reduce-scatter.13.cloned.1.call-update) | async-done | bytes 786448 | tf_op jit(solution)/shard_map/reduce_scatter | solution.py:150
  252.9 27.2 %all-gather.9.cloned.1.call-done = bf16[2048,768]{1,0:T(8,128)(2,1)} async-done(((bf16[512,768]{1,0:T(8,128)(2,1)}), bf16[2048,768]{1,0:T(8,128)(2,1)}) %all-gather.9.cloned.1.call-update) | async-done | bytes 3145744 | tf_op jit(solution)/shard_map/all_gather | solution.py:160
  287.6 36.0 %all-gather.13.cloned.1.call-done = bf16[768,768]{0,1:T(8,128)(2,1)} async-done(((bf16[768,96]{0,1:T(8,128)(2,1)}), bf16[768,768]{0,1:T(8,128)(2,1)}) %all-gather.13.cloned.1.call-update) | async-done | bytes 1179664 | tf_op jit(solution)/shard_map/all_gather | solution.py:110
  323.6 28.9 %all-gather.15.cloned.1.call-done = bf16[2048,768]{1,0:T(8,128)(2,1)} async-done(((bf16[512,768]{1,0:T(8,128)(2,1)}), bf16[2048,768]{1,0:T(8,128)(2,1)}) %all-gather.15.cloned.1.call-update) | async-done | bytes 3145744 | tf_op jit(solution)/shard_map/all_gather | solution.py:174
  352.6 10.8 %convert_reduce_fusion = (f32[768]{0:T(1024)}, bf16[2048,768]{1,0:T(8,128)(2,1)S(1)}, bf16[2048,768]{1,0:T(8,128)(2,1)}) fusion(f32[2048,768]{1,0:T(8,128)} %fusion.88, f32[768]{0:T(1024)S(1)} %dynamic_slice.28, bf16[2048,768]{1,0:T(8,128)(2,1)} %all-gather.15.cloned.1.call-done, bf16[768,768]{0,1:T(8,128)(2,1)} %all-gather.13.cloned.1.call-done), kind=kOutput, calls=%fused_computation.57 | convolution fusion | flops 2455239936 | bytes 16914432 | tf_op jit(solution)/shard_map/dot_general | solution.py:178
  376.6 30.5 %reduce-scatter.17.cloned.1.call-done = bf16[512,768]{1,0:T(8,128)(2,1)} async-done(((bf16[2048,768]{1,0:T(8,128)(2,1)}), bf16[512,768]{1,0:T(8,128)(2,1)}) %reduce-scatter.17.cloned.1.call-update) | async-done | bytes 786448 | tf_op jit(solution)/shard_map/reduce_scatter | solution.py:189
  411.1 36.4 %reduce-scatter.15.cloned.1.call-done = bf16[512,768]{1,0:T(8,128)(2,1)} async-done(((bf16[2048,768]{1,0:T(8,128)(2,1)}), bf16[512,768]{1,0:T(8,128)(2,1)}) %reduce-scatter.15.cloned.1.call-update) | async-done | bytes 786448 | tf_op jit(solution)/shard_map/reduce_scatter | solution.py:165
  454.8 28.4 %all-gather.17.cloned.1.call-done = bf16[2048,768]{1,0:T(8,128)(2,1)} async-done(((bf16[512,768]{1,0:T(8,128)(2,1)}), bf16[2048,768]{1,0:T(8,128)(2,1)}) %all-gather.17.cloned.1.call-update) | async-done | bytes 3145744 | tf_op jit(solution)/shard_map/all_gather | solution.py:208
  487.0 157.7 %while.28 = (s32[]{:T(128)}, f32[2048,3,64]{0,2,1:T(8,128)}, f32[2048,3,64]{0,2,1:T(8,128)}, f32[4,512,3,64]{1,0,3,2:T(4,128)}, bf16[4,512,3,64]{1,3,2,0:T(8,128...) while((s32[]{:T(128)}, f32[2048,3,64]{0,2,1:T(8,128)}, ...), condition=%wide.region_18.19_spmd.clone, body=%wide.region_16.18_spmd.clone.sunk | while | flops 2053634560 | bytes 151972176 | solution.py:242
  516.4 8.6 dynamic_update_slice.24
  556.3 8.6 dynamic_update_slice.24
  596.1 8.6 dynamic_update_slice.24
  635.9 8.6 dynamic_update_slice.24
  696.3 19.6 %reduce-scatter.27.cloned.1.call-done = f32[96,192]{1,0:T(8,128)} async-done(((f32[768,192]{1,0:T(8,128)}), f32[96,192]{1,0:T(8,128)}) %reduce-scatter.27.cloned.1.call-update) | async-done | bytes 73744
  717.5 68.3 %reduce-scatter.25.cloned.1.call-done = f32[96,576]{1,0:T(8,128)} async-done(((f32[768,576]{1,0:T(8,128)}), f32[96,576]{1,0:T(8,128)}) %reduce-scatter.25.cloned.1.call-update) | async-done | bytes 221200
  787.7 37.6 %reduce-scatter.19.cloned.1.call-done = bf16[512,768]{1,0:T(8,128)(2,1)} async-done(((bf16[2048,768]{1,0:T(8,128)(2,1)}), bf16[512,768]{1,0:T(8,128)(2,1)}) %reduce-scatter.19.cloned.1.call-update) | async-done | bytes 786448 | tf_op jit(solution)/shard_map/reduce_scatter | solution.py:256
  827.8 41.3 %all-reduce = (f32[768]{0:T(1024)}, f32[768]{0:T(1024)}, f32[768]{0:T(1024)}, f32[3072]{0:T(1024)}, f32[768]{0:T(1024)}, /*index=5*/f32[2304]{0:T(1024)}) all-reduce(f32[768]{0:T(1024)S(1)} %get-tuple-element.311, f32[768]{0:T(1024)S(1)} %get-tuple-element.314, ...), channel_id=1, replica_groups=mesh['dp'=8,'tensor'=4] {'dp','tensor'}, use_global_device_ids=true, to_apply=%region_23.24 | all-reduce | flops 8448 | bytes 67584 | tf_op jit(solution)/shard_map/psum | solution.py:273
  872.3 27.9 %reduce-scatter.21.cloned.1.call-done = f32[96,768]{1,0:T(8,128)} async-done(((f32[768,768]{1,0:T(8,128)}), f32[96,768]{1,0:T(8,128)}) %reduce-scatter.21.cloned.1.call-update) | async-done | bytes 294928 | tf_op jit(solution)/shard_map/reduce_scatter | solution.py:270
  900.2 73.0 %reduce-scatter.23.cloned.1.call-done = f32[768,96]{0,1:T(8,128)} async-done(((f32[768,768]{0,1:T(8,128)}), f32[768,96]{0,1:T(8,128)}) %reduce-scatter.23.cloned.1.call-update) | async-done | bytes 294928 | tf_op jit(solution)/shard_map/reduce_scatter | solution.py:271
  (341 shorter events, 349.4 us)
Async XLA Ops:
  8.0 204.3 %copy-start = (f32[128,2304]{1,0:T(8,128)S(1)}, f32[128,2304]{1,0:T(8,128)}, u32[]{:S(2)}) copy-start(f32[128,2304]{1,0:T(8,128)} %param.32) | copy-start | bytes 3538948
  8.1 83.6 %all-gather.7.cloned.1.call-start = ((), (), s32[]{:S(2)}) async-start(), calls=%async_computation.8 | async-start | bytes 3932160 | tf_op jit(solution)/shard_map/all_gather | solution.py:116
  11.6 233.2 %reduce-scatter.13.cloned.1.call-start = ((), (), s32[]{:S(2)}) async-start(), calls=%async_computation.9 | async-start | bytes 3932160 | tf_op jit(solution)/shard_map/reduce_scatter | solution.py:150
  206.9 46.0 %all-gather.11.cloned.1.call-start = ((), (), s32[]{:S(2)}) async-start(), calls=%async_computation.11 | async-start | bytes 1327104 | tf_op jit(solution)/shard_map/all_gather | solution.py:109
  208.6 71.5 %all-gather.9.cloned.1.call-start = ((), (), s32[]{:S(2)}) async-start(), calls=%async_computation.10 | async-start | bytes 3932160 | tf_op jit(solution)/shard_map/all_gather | solution.py:160
  250.6 73.1 %all-gather.13.cloned.1.call-start = ((), (), s32[]{:S(2)}) async-start(), calls=%async_computation.12 | async-start | bytes 1327104 | tf_op jit(solution)/shard_map/all_gather | solution.py:110
  251.3 101.2 %all-gather.15.cloned.1.call-start = ((), (), s32[]{:S(2)}) async-start(), calls=%async_computation.14 | async-start | bytes 3932160 | tf_op jit(solution)/shard_map/all_gather | solution.py:174
  252.1 155.1 %reduce-scatter.17.cloned.1.call-start = ((), (), s32[]{:S(2)}) async-start(), calls=%async_computation.15 | async-start | bytes 3932160 | tf_op jit(solution)/shard_map/reduce_scatter | solution.py:189
  287.6 77.4 %copy-start.57 = (bf16[768,768]{1,0:T(8,128)(2,1)S(1)}, bf16[768,768]{1,0:T(8,128)(2,1)}, u32[]{:S(2)}) copy-start(bf16[768,768]{1,0:T(8,128)(2,1)} %all-gather.11.cloned.1.call-done) | copy-start | bytes 3538948
  369.1 78.3 %reduce-scatter.15.cloned.1.call-start = ((), (), s32[]{:S(2)}) async-start(), calls=%async_computation.13 | async-start | bytes 3932160 | tf_op jit(solution)/shard_map/reduce_scatter | solution.py:165
  376.6 106.6 %all-gather.17.cloned.1.call-start = ((), (), s32[]{:S(2)}) async-start(), calls=%async_computation.16 | async-start | bytes 3932160 | tf_op jit(solution)/shard_map/all_gather | solution.py:208
  454.7 261.2 %reduce-scatter.27.cloned.1.call-start = ((), (), s32[]{:S(2)}) async-start(), calls=%async_computation.22 | async-start | bytes 884736
  652.1 133.7 %reduce-scatter.25.cloned.1.call-start = ((), (), s32[]{:S(2)}) async-start(), calls=%async_computation.21 | async-start | bytes 2211840
  666.9 158.4 %reduce-scatter.19.cloned.1.call-start = ((), (), s32[]{:S(2)}) async-start(), calls=%async_computation.17 | async-start | bytes 3932160 | tf_op jit(solution)/shard_map/reduce_scatter | solution.py:256
  674.0 226.3 %reduce-scatter.21.cloned.1.call-start = ((), (), s32[]{:S(2)}) async-start(), calls=%async_computation.18 | async-start | bytes 2654208 | tf_op jit(solution)/shard_map/reduce_scatter | solution.py:270
  681.9 291.4 %reduce-scatter.23.cloned.1.call-start = ((), (), s32[]{:S(2)}) async-start(), calls=%async_computation.19 | async-start | bytes 2654208 | tf_op jit(solution)/shard_map/reduce_scatter | solution.py:271
  689.2 284.1 %all-reduce.3.cloned.1.call-start = ((), (), s32[]{:S(2)}) async-start(), calls=%async_computation.20 | async-start | bytes 2359296 | tf_op jit(solution)/shard_map/psum | solution.py:273
  694.0 131.3 %copy-start.8 = (f32[512,768]{1,0:T(8,128)S(1)}, f32[512,768]{1,0:T(8,128)}, u32[]{:S(2)}) copy-start(f32[512,768]{1,0:T(8,128)} %param.19) | copy-start | bytes 4718596
  694.0 131.3 %copy-start.40 = (f32[512]{0:T(512)S(1)}, f32[512]{0:T(512)}, u32[]{:S(2)}) copy-start(f32[512]{0:T(512)} %copy-done.39) | copy-start | bytes 6148
  694.0 131.2 %copy-start.42 = (f32[768]{0:T(1024)S(1)}, f32[768]{0:T(1024)}, u32[]{:S(2)}) copy-start(f32[768]{0:T(1024)} %param.23) | copy-start | bytes 9220
  694.0 131.2 %copy-start.44 = (f32[512]{0:T(512)S(1)}, f32[512]{0:T(512)}, u32[]{:S(2)}) copy-start(f32[512]{0:T(512)} %copy-done.43) | copy-start | bytes 6148
  717.5 110.3 %copy-start.46 = (f32[768]{0:T(1024)S(1)}, f32[768]{0:T(1024)}, u32[]{:S(2)}) copy-start(f32[768]{0:T(1024)} %get-tuple-element.310) | copy-start | bytes 9220
  717.5 110.3 %copy-start.47 = (f32[768]{0:T(1024)S(1)}, f32[768]{0:T(1024)}, u32[]{:S(2)}) copy-start(f32[768]{0:T(1024)} %get-tuple-element.363) | copy-start | bytes 9220
  869.1 106.5 %copy-start.1 = (f32[128,2304]{1,0:T(8,128)S(1)}, f32[128,2304]{1,0:T(8,128)}, u32[]{:S(2)}) copy-start(f32[128,2304]{1,0:T(8,128)} %param.32) | copy-start | bytes 3538948
  (72 other events, 567.9 us)
Sparse Core Ops, SparseCore 0:
  11.7 31.2 all-gather.6
  207.0 37.6 reduce-scatter.12
  369.2 37.8 reduce-scatter.16
  409.5 37.8 reduce-scatter.14
  696.4 151.9 all-reduce.2
Sparse Core Ops, SparseCore 1:
  210.2 41.1 all-gather.10
  253.3 26.7 all-gather.8
  282.2 41.4 all-gather.12
  325.8 26.7 all-gather.14
  454.8 28.3 all-gather.16
  652.2 63.6 reduce-scatter.26
  719.2 66.5 reduce-scatter.24
  788.2 37.0 reduce-scatter.18
  829.2 71.0 reduce-scatter.20
  904.3 68.9 reduce-scatter.22
where the time goes:
time: 991 us; the launch traced here: 983 us
  waiting for transfers between devices  441 us (45%)
  matrix products  226 us (23%)
  blocking collectives  115 us (12%)
  other arithmetic  102 us (10%)
  local copies, waits for them, and re-layouts  79.7 us (8%)
  between operations  16.4 us (2%)
    unnamed x17, waiting for transfers between devices  88.8 us
    reduce_scatter x1, waiting for transfers between devices, shards(): lax.psum_scatter(down_part, 'dp', scatter_dimension=1, tiled=True)  73 us
    dot_general x8, matrix products, masked_scores(): jnp.einsum('qhd,khd->hqk', query_block, keys_low, preferred_element_type=...  42.3 us
    psum x1, blocking collectives, shards(): lax.psum((gain_part, bias_part, proj_bias_part, up_bias_part, down_bias_p...  41.3 us
    all_gather x1, blocking collectives, shards(): lax.all_gather(qkv_weight.astype(jnp.bfloat16), 'dp', axis=1, tiled=True)  40.6 us
    reduce_scatter x1, waiting for transfers between devices, shards(): lax.psum_scatter(jnp.einsum('cte,cde->td', qkv_grad, gathered_qkv, prefer...  37.6 us
    reduce_scatter x1, waiting for transfers between devices, shards(): lax.psum_scatter(jnp.dot(active_low, gathered_down, preferred_element_typ...  36.4 us
    dynamic_update_slice x8, local copies, waits for them, and re-layouts, shards(): lax.scan(backward_block, (empty_grad, empty_grad), (query_blocks, segment...  36 us
  transfers between devices with their start and end apart: 15, of which 12 were waited for; matrix products, arithmetic and copies ran while one was open for 9% of the time, Pallas kernels for 0%

commit v1 on v0

--- a/solution.py
+++ b/solution.py
@@ -157,7 +157,23 @@
     hidden_normed, inverse_hidden = normalize(hidden)
     modulated_low = (hidden_normed * (1.0 + mod_scale) + mod_shift).astype(jnp.bfloat16)
     branch_grad = out_grad * mod_gate
-    modulated_full = lax.all_gather(modulated_low, "tensor", axis=0, tiled=True)
+    ways, here, step = (lax.axis_size("tensor"), lax.axis_index("tensor"), modulated_low.shape[0])
+    dims = [n * ways if d == 0 else n for d, n in enumerate(modulated_low.shape)]
+    full = lax.dynamic_update_slice_in_dim(
+        jnp.zeros(dims, modulated_low.dtype), modulated_low, here * step, axis=0
+    )
+    going_up = going_down = modulated_low
+    for far in range(1, ways // 2 + 1):
+        going_up = lax.ppermute(going_up, "tensor", [(d, (d + 1) % ways) for d in range(ways)])
+        full = lax.dynamic_update_slice_in_dim(full, going_up, (here - far) % ways * step, axis=0)
+        if 2 * far < ways:
+            going_down = lax.ppermute(
+                going_down, "tensor", [(d, (d - 1) % ways) for d in range(ways)]
+            )
+            full = lax.dynamic_update_slice_in_dim(
+                full, going_down, (here + far) % ways * step, axis=0
+            )
+    modulated_full = full
     up_bias_own = lax.dynamic_slice_in_dim(up_bias, tensor_rank * local_units, local_units)
     pre_act = jnp.dot(modulated_full, gathered_up, preferred_element_type=jnp.float32) + up_bias_own
     active, gelu_pullback = jax.vjp(gelu_tanh, pre_act)

time: 991 us -> 967 us (0.976)
  waiting for transfers between devices: 441 us -> 423 us
    all_gather x1, waiting for transfers between devices: 36 us -> 0.01 us  [shards(): lax.all_gather(down_weight.astype(jnp.bfloat16), 'dp', axis=1, tiled=True)]
    all_gather x1, waiting for transfers between devices: 0.01 us -> 34 us  [shards(): lax.all_gather(up_weight.astype(jnp.bfloat16), 'dp', axis=0, tiled=True)]
    all_gather x1 -> x0, waiting for transfers between devices: 27.2 us -> none  [shards(): modulated_full = lax.all_gather(modulated_low, 'tensor', axis=0, tiled=True)]
    ppermute x0 -> x3, waiting for transfers between devices: none -> 26.4 us  [the longest x2 26.4 us: shards(): lax.ppermute(going_up, 'tensor', [(d, (d + 1) % ways) for d in range(ways)])]
    all_gather x1, waiting for transfers between devices: 28.9 us -> 12.1 us  [shards(): lax.all_gather(branch_grad.astype(jnp.bfloat16), 'tensor', axis=0, tiled=...]
    unnamed x17 -> x16, waiting for transfers between devices: 88.8 us -> 92 us
    unnamed x115 -> x125, local copies, waits for them, and re-layouts: 25.8 us -> 25.8 us
  transfers between devices with their start and end apart: 15 -> 17, of which waited for: 12 -> 12; matrix products, arithmetic and copies ran while one was open for 9% -> 9% of each run, Pallas kernels for 0% -> 0%
where the time goes in v1:
time: 967 us; the launch traced here: 959 us
  waiting for transfers between devices  423 us (44%)
  matrix products  224 us (23%)
  blocking collectives  112 us (12%)
  other arithmetic  97.6 us (10%)
  local copies, waits for them, and re-layouts  82.5 us (9%)
  between operations  16.5 us (2%)
    unnamed x16, waiting for transfers between devices  92 us
    reduce_scatter x1, waiting for transfers between devices, shards(): lax.psum_scatter(down_part, 'dp', scatter_dimension=1, tiled=True)  73 us
    dot_general x8, matrix products, masked_scores(): jnp.einsum('qhd,khd->hqk', query_block, keys_low, preferred_element_type=...  42.5 us
    psum x1, blocking collectives, shards(): lax.psum((gain_part, bias_part, proj_bias_part, up_bias_part, down_bias_p...  41.5 us
    all_gather x1, blocking collectives, shards(): lax.all_gather(qkv_weight.astype(jnp.bfloat16), 'dp', axis=1, tiled=True)  38.8 us
    reduce_scatter x1, waiting for transfers between devices, shards(): lax.psum_scatter(jnp.einsum('cte,cde->td', qkv_grad, gathered_qkv, prefer...  37.7 us
    reduce_scatter x1, waiting for transfers between devices, shards(): lax.psum_scatter(jnp.dot(active_low, gathered_down, preferred_element_typ...  36.4 us
    dynamic_update_slice x8, local copies, waits for them, and re-layouts, shards(): lax.scan(backward_block, (empty_grad, empty_grad), (query_blocks, segment...  36 us
  transfers between devices with their start and end apart: 17, of which 12 were waited for; matrix products, arithmetic and copies ran while one was open for 9% of the time, Pallas kernels for 0%

profile of v1, /device:TPU:0, one launch (start us, length us, event | category | flops | bytes accessed | tf_op | source)
XLA Modules:
  0.0 959.2 jit_solution(9266808771368937514)
XLA Ops:
  12.9 38.8 %all_gather.22 = bf16[3,768,192]{2,0,1:T(4,128)(2,1)S(1)} all-gather(bf16[3,96,192]{2,0,1:T(4,128)(2,1)S(1)} %copy.65), channel_id=1, replica_groups=mesh['dp'=8,'tensor'=4] {'dp'}, dimensions={1}, use_global_device_ids=true | all-gather | bytes 995328 | tf_op jit(solution)/shard_map/all_gather | solution.py:107
  53.8 31.1 %all_gather.23 = bf16[192,768]{0,1:T(8,128)(2,1)S(1)} all-gather(bf16[192,96]{0,1:T(8,128)(2,1)S(1)} %copy.69), channel_id=1, replica_groups=mesh['dp'=8,'tensor'=4] {'dp'}, dimensions={1}, use_global_device_ids=true | all-gather | bytes 331776 | tf_op jit(solution)/shard_map/all_gather | solution.py:108
  99.9 95.0 %while.27 = (s32[]{:T(128)}, bf16[4,512,3,64]{1,3,2,0:T(8,128)(2,1)}, f32[4,3,512]{2,1,0:T(4,128)}, s32[4,512]{1,0:T(4,128)S(1)}, s32[2048]{0:T(1024)S(1)}, /*in...) while((s32[]{:T(128)}, ...), condition=%wide.region_8.9_spmd, body=%wide.region_5.8_spmd.sunk | while | flops 834763264 | bytes 43974772 | solution.py:148
  108.4 7.8 fusion.141
  132.1 7.8 fusion.141
  210.1 27.4 %reduce-scatter.13.cloned.1.call-done = bf16[512,768]{1,0:T(8,128)(2,1)} async-done(((bf16[2048,768]{1,0:T(8,128)(2,1)}), bf16[512,768]{1,0:T(8,128)(2,1)}) %reduce-scatter.13.cloned.1.call-update) | async-done | bytes 786448 | tf_op jit(solution)/shard_map/reduce_scatter | solution.py:150
  247.2 26.4 %collective-permute-done = bf16[512,768]{1,0:T(8,128)(2,1)S(1)} collective-permute-done((bf16[512,768]{1,0:T(8,128)(2,1)}, bf16[512,768]{1,0:T(8,128)(2,1)S(1)}, u32[]{:S(2)}, u32[]{:S(2)}) %collective-permute-start) | collective-permute-done | bytes 786464 | tf_op jit(solution)/shard_map/ppermute | solution.py:167
  273.5 12.1 %all-gather.12.cloned.1.call-done = bf16[2048,768]{1,0:T(8,128)(2,1)} async-done(((bf16[512,768]{1,0:T(8,128)(2,1)}), bf16[2048,768]{1,0:T(8,128)(2,1)}) %all-gather.12.cloned.1.call-update) | async-done | bytes 3145744 | tf_op jit(solution)/shard_map/all_gather | solution.py:190
  296.0 34.0 %all-gather.8.cloned.1.call-done = bf16[768,768]{1,0:T(8,128)(2,1)} async-done(((bf16[96,768]{1,0:T(8,128)(2,1)}), bf16[768,768]{1,0:T(8,128)(2,1)}) %all-gather.8.cloned.1.call-update) | async-done | bytes 1179664 | tf_op jit(solution)/shard_map/all_gather | solution.py:109
  329.9 12.2 %convert_reduce_fusion = (f32[768]{0:T(1024)}, bf16[2048,768]{1,0:T(8,128)(2,1)S(1)}, bf16[2048,768]{1,0:T(8,128)(2,1)}) fusion(f32[2048,768]{1,0:T(8,128)} %fusion.89, f32[768]{0:T(1024)S(1)} %dynamic_slice.28, bf16[2048,768]{1,0:T(8,128)(2,1)} %constant_dynamic-update-slice_fusion, bf16[768,768]{1,0:T(8,128)(2,1)} %all-gather.8.cloned.1.call-done), kind=kOutput, calls=%fused_computation.57 | convolution fusion | flops 2455239936 | bytes 16914432 | tf_op jit(solution)/shard_map/dot_general | solution.py:178
  355.2 28.7 %reduce-scatter.17.cloned.1.call-done = bf16[512,768]{1,0:T(8,128)(2,1)} async-done(((bf16[2048,768]{1,0:T(8,128)(2,1)}), bf16[512,768]{1,0:T(8,128)(2,1)}) %reduce-scatter.17.cloned.1.call-update) | async-done | bytes 786448 | tf_op jit(solution)/shard_map/reduce_scatter | solution.py:205
  387.9 36.4 %reduce-scatter.15.cloned.1.call-done = bf16[512,768]{1,0:T(8,128)(2,1)} async-done(((bf16[2048,768]{1,0:T(8,128)(2,1)}), bf16[512,768]{1,0:T(8,128)(2,1)}) %reduce-scatter.15.cloned.1.call-update) | async-done | bytes 786448 | tf_op jit(solution)/shard_map/reduce_scatter | solution.py:181
  431.5 28.6 %all-gather.14.cloned.1.call-done = bf16[2048,768]{1,0:T(8,128)(2,1)} async-done(((bf16[512,768]{1,0:T(8,128)(2,1)}), bf16[2048,768]{1,0:T(8,128)(2,1)}) %all-gather.14.cloned.1.call-update) | async-done | bytes 3145744 | tf_op jit(solution)/shard_map/all_gather | solution.py:224
  463.9 157.7 %while.28 = (s32[]{:T(128)}, f32[2048,3,64]{0,2,1:T(8,128)}, f32[2048,3,64]{0,2,1:T(8,128)}, f32[4,512,3,64]{1,0,3,2:T(4,128)}, bf16[4,512,3,64]{1,3,2,0:T(8,128...) while((s32[]{:T(128)}, f32[2048,3,64]{0,2,1:T(8,128)}, ...), condition=%wide.region_18.19_spmd.clone, body=%wide.region_16.18_spmd.clone.sunk | while | flops 2053634560 | bytes 151972176 | solution.py:258
  493.4 8.6 dynamic_update_slice.44
  533.2 8.6 dynamic_update_slice.44
  573.1 8.6 dynamic_update_slice.44
  612.9 8.6 dynamic_update_slice.44
  669.1 23.5 %reduce-scatter.27.cloned.1.call-done = f32[96,192]{1,0:T(8,128)} async-done(((f32[768,192]{1,0:T(8,128)}), f32[96,192]{1,0:T(8,128)}) %reduce-scatter.27.cloned.1.call-update) | async-done | bytes 73744
  694.3 68.3 %reduce-scatter.25.cloned.1.call-done = f32[96,576]{1,0:T(8,128)} async-done(((f32[768,576]{1,0:T(8,128)}), f32[96,576]{1,0:T(8,128)}) %reduce-scatter.25.cloned.1.call-update) | async-done | bytes 221200
  764.5 37.7 %reduce-scatter.19.cloned.1.call-done = bf16[512,768]{1,0:T(8,128)(2,1)} async-done(((bf16[2048,768]{1,0:T(8,128)(2,1)}), bf16[512,768]{1,0:T(8,128)(2,1)}) %reduce-scatter.19.cloned.1.call-update) | async-done | bytes 786448 | tf_op jit(solution)/shard_map/reduce_scatter | solution.py:272
  804.8 41.5 %all-reduce = (f32[768]{0:T(1024)}, f32[768]{0:T(1024)}, f32[768]{0:T(1024)}, f32[3072]{0:T(1024)}, f32[768]{0:T(1024)}, /*index=5*/f32[2304]{0:T(1024)}) all-reduce(f32[768]{0:T(1024)S(1)} %get-tuple-element.311, f32[768]{0:T(1024)S(1)} %get-tuple-element.314, ...), channel_id=1, replica_groups=mesh['dp'=8,'tensor'=4] {'dp','tensor'}, use_global_device_ids=true, to_apply=%region_23.24 | all-reduce | flops 8448 | bytes 67584 | tf_op jit(solution)/shard_map/psum | solution.py:289
  849.5 26.8 %reduce-scatter.21.cloned.1.call-done = f32[96,768]{1,0:T(8,128)} async-done(((f32[768,768]{1,0:T(8,128)}), f32[96,768]{1,0:T(8,128)}) %reduce-scatter.21.cloned.1.call-update) | async-done | bytes 294928 | tf_op jit(solution)/shard_map/reduce_scatter | solution.py:286
  876.3 73.0 %reduce-scatter.23.cloned.1.call-done = f32[768,96]{0,1:T(8,128)} async-done(((f32[768,768]{0,1:T(8,128)}), f32[768,96]{0,1:T(8,128)}) %reduce-scatter.23.cloned.1.call-update) | async-done | bytes 294928 | tf_op jit(solution)/shard_map/reduce_scatter | solution.py:287
  (351 shorter events, 345.3 us)
Async XLA Ops:
  8.0 195.1 %copy-start = (f32[128,2304]{1,0:T(8,128)S(1)}, f32[128,2304]{1,0:T(8,128)}, u32[]{:S(2)}) copy-start(f32[128,2304]{1,0:T(8,128)} %param.32) | copy-start | bytes 3538948
  8.1 78.7 %all-gather.6.cloned.1.call-start = ((), (), s32[]{:S(2)}) async-start(), calls=%async_computation.8 | async-start | bytes 3932160 | tf_op jit(solution)/shard_map/all_gather | solution.py:116
  11.6 226.0 %reduce-scatter.13.cloned.1.call-start = ((), (), s32[]{:S(2)}) async-start(), calls=%async_computation.9 | async-start | bytes 3932160 | tf_op jit(solution)/shard_map/reduce_scatter | solution.py:150
  200.7 72.8 %all-gather.10.cloned.1.call-start = ((), (), s32[]{:S(2)}) async-start(), calls=%async_computation.11 | async-start | bytes 1327104 | tf_op jit(solution)/shard_map/all_gather | solution.py:110
  202.3 83.3 %all-gather.12.cloned.1.call-start = ((), (), s32[]{:S(2)}) async-start(), calls=%async_computation.13 | async-start | bytes 3932160 | tf_op jit(solution)/shard_map/all_gather | solution.py:190
  209.3 120.6 %all-gather.8.cloned.1.call-start = ((), (), s32[]{:S(2)}) async-start(), calls=%async_computation.10 | async-start | bytes 1327104 | tf_op jit(solution)/shard_map/all_gather | solution.py:109
  210.1 173.9 %reduce-scatter.17.cloned.1.call-start = ((), (), s32[]{:S(2)}) async-start(), calls=%async_computation.14 | async-start | bytes 3932160 | tf_op jit(solution)/shard_map/reduce_scatter | solution.py:205
  244.6 28.9 %collective-permute-start = (bf16[512,768]{1,0:T(8,128)(2,1)}, bf16[512,768]{1,0:T(8,128)(2,1)S(1)}, u32[]{:S(2)}, u32[]{:S(2)}) collective-permute-start(bf16[512,768]{1,0:T(8,128)(2,1)} %get-tuple-element.366), channel_id=1, source_target_pairs={{0,1},{1,2},{2,3},{3,0},{4,5},{5,6},{6,7},{7,4},{8,9},{9,10},{10,1... | collective-permute-start | bytes 2359304 | tf_op jit(solution)/shard_map/ppermute | solution.py:167
  244.6 49.4 %collective-permute-start.1 = (bf16[512,768]{1,0:T(8,128)(2,1)}, bf16[512,768]{1,0:T(8,128)(2,1)S(1)}, u32[]{:S(2)}, u32[]{:S(2)}) collective-permute-start(bf16[512,768]{1,0:T(8,128)(2,1)} %get-tuple-element.366), channel_id=1, source_target_pairs={{0,3},{1,0},{2,1},{3,2},{4,7},{5,4},{6,5},{7,6},{8,11},{9,8},{10,9... | collective-permute-start | bytes 2359304 | tf_op jit(solution)/shard_map/ppermute | solution.py:170
  273.5 21.5 %collective-permute-start.2 = (bf16[512,768]{1,0:T(8,128)(2,1)S(1)}, bf16[512,768]{1,0:T(8,128)(2,1)S(1)}, u32[]{:S(2)}, u32[]{:S(2)}) collective-permute-start(bf16[512,768]{1,0:T(8,128)(2,1)S(1)} %collective-permute-done), channel_id=1, source_target_pairs={{0,1},{1,2},{2,3},{3,0},{4,5},{5,6},{6,7},{7,4},{8,9},{9,10},{10,1... | collective-permute-start | bytes 2359304 | tf_op jit(solution)/shard_map/ppermute | solution.py:167
  347.7 76.5 %reduce-scatter.15.cloned.1.call-start = ((), (), s32[]{:S(2)}) async-start(), calls=%async_computation.12 | async-start | bytes 3932160 | tf_op jit(solution)/shard_map/reduce_scatter | solution.py:181
  355.2 104.9 %all-gather.14.cloned.1.call-start = ((), (), s32[]{:S(2)}) async-start(), calls=%async_computation.15 | async-start | bytes 3932160 | tf_op jit(solution)/shard_map/all_gather | solution.py:224
  431.5 261.2 %reduce-scatter.27.cloned.1.call-start = ((), (), s32[]{:S(2)}) async-start(), calls=%async_computation.21 | async-start | bytes 884736
  629.1 133.5 %reduce-scatter.25.cloned.1.call-start = ((), (), s32[]{:S(2)}) async-start(), calls=%async_computation.20 | async-start | bytes 2211840
  642.6 159.5 %reduce-scatter.19.cloned.1.call-start = ((), (), s32[]{:S(2)}) async-start(), calls=%async_computation.16 | async-start | bytes 3932160 | tf_op jit(solution)/shard_map/reduce_scatter | solution.py:272
  649.0 227.3 %reduce-scatter.21.cloned.1.call-start = ((), (), s32[]{:S(2)}) async-start(), calls=%async_computation.17 | async-start | bytes 2654208 | tf_op jit(solution)/shard_map/reduce_scatter | solution.py:286
  656.2 293.1 %reduce-scatter.23.cloned.1.call-start = ((), (), s32[]{:S(2)}) async-start(), calls=%async_computation.18 | async-start | bytes 2654208 | tf_op jit(solution)/shard_map/reduce_scatter | solution.py:287
  662.5 286.8 %all-reduce.3.cloned.1.call-start = ((), (), s32[]{:S(2)}) async-start(), calls=%async_computation.19 | async-start | bytes 2359296 | tf_op jit(solution)/shard_map/psum | solution.py:289
  666.8 135.3 %copy-start.9 = (f32[512,768]{1,0:T(8,128)S(1)}, f32[512,768]{1,0:T(8,128)}, u32[]{:S(2)}) copy-start(f32[512,768]{1,0:T(8,128)} %param.19) | copy-start | bytes 4718596
  666.8 135.3 %copy-start.42 = (f32[512]{0:T(512)S(1)}, f32[512]{0:T(512)}, u32[]{:S(2)}) copy-start(f32[512]{0:T(512)} %copy-done.41) | copy-start | bytes 6148
  666.9 135.3 %copy-start.44 = (f32[768]{0:T(1024)S(1)}, f32[768]{0:T(1024)}, u32[]{:S(2)}) copy-start(f32[768]{0:T(1024)} %param.23) | copy-start | bytes 9220
  666.9 135.3 %copy-start.46 = (f32[512]{0:T(512)S(1)}, f32[512]{0:T(512)}, u32[]{:S(2)}) copy-start(f32[512]{0:T(512)} %copy-done.45) | copy-start | bytes 6148
  669.1 135.6 %copy-start.48 = (f32[768]{0:T(1024)S(1)}, f32[768]{0:T(1024)}, u32[]{:S(2)}) copy-start(f32[768]{0:T(1024)} %get-tuple-element.310) | copy-start | bytes 9220
  669.1 135.6 %copy-start.49 = (f32[768]{0:T(1024)S(1)}, f32[768]{0:T(1024)}, u32[]{:S(2)}) copy-start(f32[768]{0:T(1024)} %get-tuple-element.363) | copy-start | bytes 9220
  (75 other events, 838.4 us)
Sparse Core Ops, SparseCore 0:
  11.7 31.2 all-gather.5
  200.8 36.7 reduce-scatter.12
  431.6 28.4 all-gather.13
  669.3 151.9 all-reduce.2
Sparse Core Ops, SparseCore 1:
  203.9 40.2 all-gather.9
  246.2 39.3 all-gather.11
  287.6 42.2 all-gather.7
  347.8 36.1 reduce-scatter.16
  386.5 37.7 reduce-scatter.14
  629.2 63.4 reduce-scatter.26
  696.0 66.5 reduce-scatter.24
  765.0 37.1 reduce-scatter.18
  806.1 70.1 reduce-scatter.20
  880.3 68.9 reduce-scatter.22
